TPU v7x, 32 devices: a whole 2x2x4 slice. The times are simulated.
32 devices in a mesh: gx: 4 (over y, x), gy: 8 (over z, core).
Axes of the slice: x: 2, y: 2, z: 4, core: 2. Of those that a mesh axis runs over, the one named last changes fastest.
Arguments:
- positions: float32 [3, 262144], P(None, ('gx', 'gy')), may hold values from -6 to 6
- velocities: float32 [3, 262144], P(None, ('gx', 'gy')), may hold values from -4 to 4
- masses: float32 [262144], P(('gx', 'gy')), may hold values from 0.005 to 0.05
- long_kick: float32 [3, 262144], P(None, ('gx', 'gy')), may hold values from -3 to 3
- leaf_lists: int32 [8, 2048], P(None, ('gx', 'gy')), may hold values from 0 to 135, as said below
- ghost_ids: int32 [256], P(('gx', 'gy')), may hold values from 0 to 63, as said below
- leaf_counts: int32 [32], P(('gx', 'gy')), may hold values from 1 to 64, as said below
Outputs:
- new_positions: float32 [3, 262144], P(None, ('gx', 'gy'))
- new_velocities: float32 [3, 262144], P(None, ('gx', 'gy'))
Inputs may be any that keep to these rules, and one draw needn't show every extreme that they name: leaf_counts of a domain is at least 1; the counts of domains (i, j) and (i, j + 4) for j below 4 sum to at most 80, and some pair reaches it with one count equal to 64. `leaf_lists`: every entry below 64 is below the count of its domain; entries from 64 on name pool ghost leaves. `ghost_ids`: each id is below the count of its domain; ids may repeat.
All inputs are finite; a program needn't handle non-finite values.
Results may differ from a plain program's by a relative error of at most 0.00011.
Values sent between devices are 32-bit elements; how exact they have to be, the bound alone decides.
A program may use at most 64 MiB of HBM per device.

v0:
```python
import functools

import jax
import jax.numpy as jnp
from jax import lax
from jax.experimental import pallas as pl
from jax.experimental.pallas import tpu as pltpu
from jax.sharding import PartitionSpec as P

SUBCYCLES = 4

soften_sq = 0.04
cutoff_sq = 9.0
time_step = 0.5

MESH = pl.DeviceIdType.MESH
PAIR_ROWS = 32
SUM_ROWS = 16
ROWS = PAIR_ROWS + SUM_ROWS
WAYS = [(a, b) for a in (-1, 0, 1) for b in (-1, 0, 1)]
BESIDE = [way for way in WAYS if way != (0, 0)]
LOW_PART = True
UNROLL = 4


def thirds(value):
    first = value.astype(jnp.bfloat16).astype(jnp.float32)
    rest = value - first
    second = rest.astype(jnp.bfloat16).astype(jnp.float32)
    return first, second, rest - second


def slot_of(a, b):
    return (a + 1) * 3 + b + 1


def kernel(
    sizes, p_in, v_in, mass, kick, live_in, lists, ghosts, p, v,
    wide, pool, targets, turned, sums, ghost_sums, ghost_v, ghost_kick, sent, got, send_sem, recv_sem,
):
    nx, ny = sizes
    leaves, lanes = mass.shape
    entries = lists.shape[0]
    lent = ghosts.shape[0]
    slots = wide.shape[0] // ROWS
    me_x, me_y = lax.axis_index("gx"), lax.axis_index("gy")

    def device(a, b):
        return (lax.rem(me_x + (a + nx), nx), lax.rem(me_y + (b + ny), ny))

    barrier = pltpu.get_barrier_semaphore()
    for a, b in BESIDE:
        pl.semaphore_signal(barrier, inc=1, device_id=device(a, b), device_id_type=MESH)

    p[...] = p_in[...]
    v[...] = v_in[...]
    for g in range(lent):
        leaf = ghosts[g]
        for c in range(3):
            sent[0, c, g] = p_in[c, leaf]
            ghost_v[c, g] = v_in[c, leaf]
            ghost_kick[c, g] = kick[c, leaf]
        row = mass[leaf]
        for k in range(SUBCYCLES):
            sent[k, 3, g] = row

    def copies(k):
        made = []
        for a, b in BESIDE:
            made.append(
                pltpu.make_async_remote_copy(
                    src_ref=sent.at[k],
                    dst_ref=got.at[k, slot_of(-a, -b)],
                    send_sem=send_sem.at[k, slot_of(a, b)],
                    recv_sem=recv_sem.at[k, slot_of(-a, -b)],
                    device_id=device(a, b),
                    device_id_type=MESH,
                )
            )
        return made

    flying = []
    pl.semaphore_wait(barrier, len(BESIDE))
    flying.append(copies(0))
    for copy in flying[0]:
        copy.start()

    def put(ref, height, base, total, row, value):
        ref[pl.ds(base * height + row, total, stride=height), :] = value

    ones = jnp.ones((slots, lanes), jnp.float32)
    zeros = jnp.zeros((slots, lanes), jnp.float32)
    for row in range(18, 21):
        put(targets, PAIR_ROWS, 0, leaves, row, ones[:leaves])
    for row in range(21, 24):
        put(wide, ROWS, 0, slots, row, ones)
    for row in range(24, PAIR_ROWS):
        put(wide, ROWS, 0, slots, row, zeros)
        put(targets, PAIR_ROWS, 0, leaves, row, zeros[:leaves])
    for row in range(PAIR_ROWS + 12, ROWS):
        put(wide, ROWS, 0, slots, row, zeros)

    def lay_out(base, total, place, weight):
        norm = None
        splits = []
        for c in range(3):
            scaled = place[c] * (cutoff_sq**-0.5)
            square = scaled * scaled
            norm = square if norm is None else norm + square
            one, two, three = thirds(scaled)
            splits.append((one, two, three))
            for row, value in enumerate((one, two, one, three, one, two)):
                put(wide, ROWS, base, total, c * 6 + row, value)
        for row, value in enumerate(thirds(-norm)):
            put(wide, ROWS, base, total, 18 + row, value)
        scaled_weight = weight * (cutoff_sq**-1.5)
        moments = [scaled_weight] + [scaled_weight * place[c] for c in range(3)]
        for c, moment in enumerate(moments):
            for row, value in enumerate(thirds(moment)):
                put(wide, ROWS, base, total, PAIR_ROWS + c * 3 + row, value)
        return splits, norm

    def leaf_sums(leaf, out, where):
        target = turned[leaf]
        total = jnp.zeros((lanes, SUM_ROWS), jnp.float32)
        for j in range(0, entries, 2):
            tiles = [pool[lists[e, leaf]] for e in range(j, min(j + 2, entries))]
            near = jnp.concatenate([tile[:PAIR_ROWS] for tile in tiles], axis=1)
            carry = jnp.concatenate([tile[PAIR_ROWS:] for tile in tiles], axis=1)
            inside = jnp.dot(target, near, preferred_element_type=jnp.float32)
            apart = jnp.maximum(
                (1.0 + soften_sq / cutoff_sq) - inside, soften_sq / cutoff_sq
            )
            inverse = lax.rsqrt(apart)
            taper = jnp.maximum(inside, 0.0) * inverse
            weight = taper * taper * inverse
            high = weight.astype(jnp.bfloat16)
            contract = (((1,), (1,)), ((), ()))
            total += lax.dot_general(high, carry, contract, preferred_element_type=jnp.float32)
            if LOW_PART:
                low = (weight - high.astype(jnp.float32)).astype(jnp.bfloat16)
                total += lax.dot_general(low, carry, contract, preferred_element_type=jnp.float32)
        out[pl.ds(pl.multiple_of(where * SUM_ROWS, SUM_ROWS), SUM_ROWS), :] = total.T

    def gathered(ref, total):
        parts = []
        for c in range(4):
            rows = [ref[pl.ds(c * 3 + r, total, stride=SUM_ROWS), :] for r in range(3)]
            parts.append(rows[0] + (rows[1] + rows[2]))
        return parts

    live = time_step * live_in[...]

    for k in range(SUBCYCLES):
        splits, norm = lay_out(0, leaves, [p[c] for c in range(3)], mass[...])
        for c in range(3):
            one, two, three = [2.0 * part for part in splits[c]]
            for row, value in enumerate((one, one, two, one, three, two)):
                put(targets, PAIR_ROWS, 0, leaves, c * 6 + row, value)
        for row, value in enumerate(thirds(1.0 - norm)):
            put(targets, PAIR_ROWS, 0, leaves, 21 + row, value)
        lay_out(
            leaves + slot_of(0, 0) * lent, lent, [sent[k, c] for c in range(3)], sent[k, 3]
        )
        for copy in flying[k]:
            copy.wait_recv()
        for a, b in BESIDE:
            at = slot_of(a, b)
            lay_out(leaves + at * lent, lent, [got[k, at, c] for c in range(3)], got[k, at, 3])

        step = 8

        def narrow(i, carry):
            rows = pl.ds(pl.multiple_of(i * (step * ROWS), step * ROWS), step * ROWS)
            tiles = wide[rows, :].astype(jnp.bfloat16).reshape(step, ROWS, lanes)
            pool[pl.ds(i * step, step)] = tiles
            return carry

        lax.fori_loop(0, slots // step, narrow, 0)

        def turn(i, carry):
            for u in range(4):
                leaf = i * 4 + u
                rows = pl.ds(pl.multiple_of(leaf * PAIR_ROWS, PAIR_ROWS), PAIR_ROWS)
                turned[leaf] = targets[rows, :].T.astype(jnp.bfloat16)
            return carry

        lax.fori_loop(0, leaves // 4, turn, 0)

        if k + 1 < SUBCYCLES:

            def lend(i, carry):
                for u in range(UNROLL):
                    g = i * UNROLL + u
                    leaf_sums(ghosts[g], ghost_sums, g)
                return carry

            lax.fori_loop(0, lent // UNROLL, lend, 0)
            total, *moments = gathered(ghost_sums, lent)
            for c in range(3):
                place = sent[k, c]
                accel = moments[c] - total * place
                speed = ghost_v[c] + time_step * (accel + ghost_kick[c])
                ghost_v[c] = speed
                sent[k + 1, c] = place + time_step * speed
            flying.append(copies(k + 1))
            for copy in flying[k + 1]:
                copy.start()

        def pull(i, carry):
            for u in range(UNROLL):
                leaf = i * UNROLL + u
                leaf_sums(leaf, sums, leaf)
            return carry

        lax.fori_loop(0, leaves // UNROLL, pull, 0)
        total, *moments = gathered(sums, leaves)
        for c in range(3):
            place, speed = p[c], v[c]
            accel = moments[c] - total * place
            faster = speed + live * (accel + kick[c])
            v[c] = faster
            p[c] = place + live * faster

    for made in flying:
        for copy in made:
            copy.wait_send()


def solution(mesh):
    sizes = (mesh.shape["gx"], mesh.shape["gy"])

    def body(positions, velocities, masses, long_kick, leaf_lists, ghost_ids, leaf_counts):
        leaves = leaf_lists.shape[1]
        lanes = masses.shape[0] // leaves
        lent = ghost_ids.shape[0]
        slots = leaves + len(WAYS) * lent
        state = jax.ShapeDtypeStruct((3, leaves, lanes), jnp.float32)
        live = (jnp.arange(leaves)[:, None] < leaf_counts).astype(jnp.float32)
        live = jnp.broadcast_to(live, (leaves, lanes))
        vmem = pl.BlockSpec(memory_space=pltpu.VMEM)
        smem = pl.BlockSpec(memory_space=pltpu.SMEM)
        f32 = jnp.float32
        places, speeds = pl.pallas_call(
            functools.partial(kernel, sizes),
            out_shape=(state, state),
            in_specs=[vmem] * 5 + [smem] * 2,
            out_specs=(vmem, vmem),
            scratch_shapes=[
                pltpu.VMEM((slots * ROWS, lanes), f32),
                pltpu.VMEM((slots, ROWS, lanes), jnp.bfloat16),
                pltpu.VMEM((leaves * PAIR_ROWS, lanes), f32),
                pltpu.VMEM((leaves, lanes, PAIR_ROWS), jnp.bfloat16),
                pltpu.VMEM((leaves * SUM_ROWS, lanes), f32),
                pltpu.VMEM((lent * SUM_ROWS, lanes), f32),
                pltpu.VMEM((3, lent, lanes), f32),
                pltpu.VMEM((3, lent, lanes), f32),
                pltpu.VMEM((SUBCYCLES, 4, lent, lanes), f32),
                pltpu.VMEM((SUBCYCLES, len(WAYS), 4, lent, lanes), f32),
                pltpu.SemaphoreType.DMA((SUBCYCLES, len(WAYS))),
                pltpu.SemaphoreType.DMA((SUBCYCLES, len(WAYS))),
            ],
            compiler_params=pltpu.CompilerParams(collective_id=0, has_side_effects=True),
        )(
            positions.reshape(3, leaves, lanes),
            velocities.reshape(3, leaves, lanes),
            masses.reshape(leaves, lanes),
            long_kick.reshape(3, leaves, lanes),
            live,
            leaf_lists,
            ghost_ids,
        )
        return places.reshape(3, -1), speeds.reshape(3, -1)

    return jax.shard_map(
        body,
        mesh=mesh,
        in_specs=(
            P(None, ("gx", "gy")),
            P(None, ("gx", "gy")),
            P(("gx", "gy")),
            P(None, ("gx", "gy")),
            P(None, ("gx", "gy")),
            P(("gx", "gy")),
            P(("gx", "gy")),
        ),
        out_specs=(P(None, ("gx", "gy")), P(None, ("gx", "gy"))),
        check_vma=False,
    )
```

profile of v0, /device:TPU:0, one launch (start us, length us, event | category | flops | bytes accessed | tf_op | source)
XLA Modules:
  0.0 147.7 jit_solution(10301127701671915753)
XLA Ops:
  1.3 0.0 copy-start
  1.3 0.0 copy-start.1
  1.3 0.7 broadcast_in_dim.2.live_in
  2.0 1.6 %copy.21 = f32[1,3,64,128]{3,2,1,0:T(8,128)} copy(f32[1,3,64,128]{3,1,2,0:T(4,128)} %bitcast.24) | data formatting | bytes 196608
  3.5 0.0 copy-done
  3.5 0.0 copy-done.1
  3.5 0.7 copy_bitcast_fusion.2
  4.2 141.0 %shard_map.86 = (f32[3,64,128]{2,1,0:T(8,128)}, f32[3,64,128]{2,1,0:T(8,128)}) custom-call(f32[3,64,128]{2,1,0:T(8,128)} %bitcast.21, f32[3,64,128]{2,1,0:T(8,128)} %get-tuple-element.7.v_in, f32[64,128]{1,0:T(8,128)} %bitcast.29, f32[3,64,128]{2,1,0:T(8,128)} %get-tuple-element.6.kick, f32[64,128]{1,0:T(8,128)} %broadcast_in_dim.2.live_in, s32[8,64]{1,0:T(8,128)} %lists.1, ...), custom_call_target="tpu_custom_call" | custom-call | tf_op jit(solution)/shard_map/pallas_call | solution.py:244
  145.3 0.0 copy-start.2
  145.3 1.7 %copy.19 = f32[1,3,64,128]{3,1,2,0:T(4,128)} copy(f32[1,3,64,128]{3,2,1,0:T(8,128)} %bitcast.28) | data formatting | bytes 196608
  146.9 0.0 copy-done.2
  146.9 0.7 copy.20
  (1 shorter events, 0.0 us)
Async XLA Ops:
  1.3 2.3 %copy-start = (f32[3,8192]{1,0:T(4,128)S(1)}, f32[3,8192]{1,0:T(4,128)}, u32[]{:S(2)}) copy-start(f32[3,8192]{1,0:T(4,128)} %param.10) | copy-start | bytes 294916
  1.3 2.2 %copy-start.1 = (f32[3,8192]{1,0:T(4,128)S(1)}, f32[3,8192]{1,0:T(4,128)}, u32[]{:S(2)}) copy-start(f32[3,8192]{1,0:T(4,128)} %param.8) | copy-start | bytes 294916
  145.3 1.7 %copy-start.2 = (f32[3,64,128]{2,1,0:T(8,128)S(1)}, f32[3,64,128]{2,1,0:T(8,128)}, u32[]{:S(2)}) copy-start(f32[3,64,128]{2,1,0:T(8,128)} %get-tuple-element.4) | copy-start | bytes 294916
where the time goes:
time: 148 us
  Pallas kernels  141 us (95%)
  local copies, waits for them, and re-layouts  5.31 us (4%)
    pallas_call x1, Pallas kernels, body(): pl.pallas_call(functools.partial(kernel, sizes), out_shape=(state, state)...  141 us
    unnamed x9, local copies, waits for them, and re-layouts  3.94 us

commit v1 on v0

--- a/solution.py
+++ b/solution.py
@@ -16,11 +16,11 @@
 MESH = pl.DeviceIdType.MESH
 PAIR_ROWS = 32
 SUM_ROWS = 16
-ROWS = PAIR_ROWS + SUM_ROWS
 WAYS = [(a, b) for a in (-1, 0, 1) for b in (-1, 0, 1)]
 BESIDE = [way for way in WAYS if way != (0, 0)]
-LOW_PART = True
-UNROLL = 4
+UNROLL = 16
+GROUP = 4
+ROUND_UP = 1.0 + 2.0**-22
 
 
 def thirds(value):
@@ -36,13 +36,14 @@
 
 def kernel(
     sizes, p_in, v_in, mass, kick, live_in, lists, ghosts, p, v,
-    wide, pool, targets, turned, sums, ghost_sums, ghost_v, ghost_kick, sent, got, send_sem, recv_sem,
+    wide, heavy, pool, carry, targets, narrow, sums, ghost_sums, ghost_v, ghost_kick, sent, got,
+    send_sem, recv_sem,
 ):
     nx, ny = sizes
     leaves, lanes = mass.shape
     entries = lists.shape[0]
     lent = ghosts.shape[0]
-    slots = wide.shape[0] // ROWS
+    slots = wide.shape[0] // PAIR_ROWS
     me_x, me_y = lax.axis_index("gx"), lax.axis_index("gy")
 
     def device(a, b):
@@ -93,12 +94,12 @@
     for row in range(18, 21):
         put(targets, PAIR_ROWS, 0, leaves, row, ones[:leaves])
     for row in range(21, 24):
-        put(wide, ROWS, 0, slots, row, ones)
+        put(wide, PAIR_ROWS, 0, slots, row, ones)
     for row in range(24, PAIR_ROWS):
-        put(wide, ROWS, 0, slots, row, zeros)
+        put(wide, PAIR_ROWS, 0, slots, row, zeros)
         put(targets, PAIR_ROWS, 0, leaves, row, zeros[:leaves])
-    for row in range(PAIR_ROWS + 12, ROWS):
-        put(wide, ROWS, 0, slots, row, zeros)
+    for row in range(12, SUM_ROWS):
+        put(heavy, SUM_ROWS, 0, slots, row, zeros)
 
     def lay_out(base, total, place, weight):
         norm = None
@@ -110,37 +111,50 @@
             one, two, three = thirds(scaled)
             splits.append((one, two, three))
             for row, value in enumerate((one, two, one, three, one, two)):
-                put(wide, ROWS, base, total, c * 6 + row, value)
+                put(wide, PAIR_ROWS, base, total, c * 6 + row, value)
+        norm = norm * ROUND_UP
         for row, value in enumerate(thirds(-norm)):
-            put(wide, ROWS, base, total, 18 + row, value)
+            put(wide, PAIR_ROWS, base, total, 18 + row, value)
         scaled_weight = weight * (cutoff_sq**-1.5)
         moments = [scaled_weight] + [scaled_weight * place[c] for c in range(3)]
         for c, moment in enumerate(moments):
             for row, value in enumerate(thirds(moment)):
-                put(wide, ROWS, base, total, PAIR_ROWS + c * 3 + row, value)
+                put(heavy, SUM_ROWS, base, total, c * 3 + row, value)
         return splits, norm
 
+    blank = jnp.zeros((lanes, lanes), jnp.bfloat16)
+
     def leaf_sums(leaf, out, where):
-        target = turned[leaf]
-        total = jnp.zeros((lanes, SUM_ROWS), jnp.float32)
+        near = [lists[e, leaf] for e in range(entries)]
+        target = jnp.concatenate([narrow[leaf]] * GROUP, axis=0)
+        pair = jnp.concatenate(
+            [
+                jnp.concatenate([target, blank], axis=1),
+                jnp.concatenate([blank, target], axis=1),
+            ],
+            axis=0,
+        )
+        total = None
         for j in range(0, entries, 2):
-            tiles = [pool[lists[e, leaf]] for e in range(j, min(j + 2, entries))]
-            near = jnp.concatenate([tile[:PAIR_ROWS] for tile in tiles], axis=1)
-            carry = jnp.concatenate([tile[PAIR_ROWS:] for tile in tiles], axis=1)
-            inside = jnp.dot(target, near, preferred_element_type=jnp.float32)
-            apart = jnp.maximum(
-                (1.0 + soften_sq / cutoff_sq) - inside, soften_sq / cutoff_sq
+            source = jnp.concatenate([pool[near[j]], pool[near[j + 1]]], axis=1)
+            inside = jnp.dot(source, pair, preferred_element_type=jnp.float32)
+            rows = []
+            for half in range(2):
+                close = inside[:, half * lanes : (half + 1) * lanes]
+                inverse = lax.rsqrt((1.0 + soften_sq / cutoff_sq) - close)
+                taper = jnp.maximum(close * inverse, 0.0)
+                weight = taper * taper * inverse
+                high = weight.astype(jnp.bfloat16)
+                low = (weight - high.astype(jnp.float32)).astype(jnp.bfloat16)
+                rows.append(jnp.concatenate([high, low], axis=1))
+            moments = jnp.concatenate([carry[near[j]], carry[near[j + 1]]], axis=1)
+            part = jnp.dot(
+                moments, jnp.concatenate(rows, axis=0), preferred_element_type=jnp.float32
             )
-            inverse = lax.rsqrt(apart)
-            taper = jnp.maximum(inside, 0.0) * inverse
-            weight = taper * taper * inverse
-            high = weight.astype(jnp.bfloat16)
-            contract = (((1,), (1,)), ((), ()))
-            total += lax.dot_general(high, carry, contract, preferred_element_type=jnp.float32)
-            if LOW_PART:
-                low = (weight - high.astype(jnp.float32)).astype(jnp.bfloat16)
-                total += lax.dot_general(low, carry, contract, preferred_element_type=jnp.float32)
-        out[pl.ds(pl.multiple_of(where * SUM_ROWS, SUM_ROWS), SUM_ROWS), :] = total.T
+            total = part if total is None else total + part
+        out[pl.ds(pl.multiple_of(where * SUM_ROWS, SUM_ROWS), SUM_ROWS), :] = (
+            total[:, :lanes] + total[:, lanes:]
+        )
 
     def gathered(ref, total):
         parts = []
@@ -168,34 +182,33 @@
             at = slot_of(a, b)
             lay_out(leaves + at * lent, lent, [got[k, at, c] for c in range(3)], got[k, at, 3])
 
-        step = 8
-
-        def narrow(i, carry):
-            rows = pl.ds(pl.multiple_of(i * (step * ROWS), step * ROWS), step * ROWS)
-            tiles = wide[rows, :].astype(jnp.bfloat16).reshape(step, ROWS, lanes)
-            pool[pl.ds(i * step, step)] = tiles
-            return carry
-
-        lax.fori_loop(0, slots // step, narrow, 0)
-
-        def turn(i, carry):
-            for u in range(4):
-                leaf = i * 4 + u
-                rows = pl.ds(pl.multiple_of(leaf * PAIR_ROWS, PAIR_ROWS), PAIR_ROWS)
-                turned[leaf] = targets[rows, :].T.astype(jnp.bfloat16)
-            return carry
-
-        lax.fori_loop(0, leaves // 4, turn, 0)
+        spot = lax.broadcasted_iota(jnp.int32, (lanes, lanes), 1) // PAIR_ROWS
+        keep = [(spot == g).astype(jnp.float32).astype(jnp.bfloat16) for g in range(GROUP)]
+
+        def turn(i, _):
+            rows = pl.ds(pl.multiple_of(i * lanes, lanes), lanes)
+            block = wide[rows, :].T.astype(jnp.bfloat16)
+            for g in range(GROUP):
+                pool[i * GROUP + g] = block * keep[g]
+            rows = pl.ds(pl.multiple_of(i * (GROUP * SUM_ROWS), GROUP * SUM_ROWS), GROUP * SUM_ROWS)
+            tiles = heavy[rows, :].astype(jnp.bfloat16).reshape(GROUP, SUM_ROWS, lanes)
+            carry[pl.ds(i * GROUP, GROUP)] = tiles
+            return _
+
+        lax.fori_loop(0, slots // GROUP, turn, 0)
+
+        def shrink(i, _):
+            rows = pl.ds(pl.multiple_of(i * lanes, lanes), lanes)
+            tiles = targets[rows, :].astype(jnp.bfloat16).reshape(GROUP, PAIR_ROWS, lanes)
+            narrow[pl.ds(i * GROUP, GROUP)] = tiles
+            return _
+
+        lax.fori_loop(0, leaves // GROUP, shrink, 0)
 
         if k + 1 < SUBCYCLES:
 
-            def lend(i, carry):
-                for u in range(UNROLL):
-                    g = i * UNROLL + u
-                    leaf_sums(ghosts[g], ghost_sums, g)
-                return carry
-
-            lax.fori_loop(0, lent // UNROLL, lend, 0)
+            for g in range(lent):
+                leaf_sums(ghosts[g], ghost_sums, g)
             total, *moments = gathered(ghost_sums, lent)
             for c in range(3):
                 place = sent[k, c]
@@ -207,11 +220,11 @@
             for copy in flying[k + 1]:
                 copy.start()
 
-        def pull(i, carry):
+        def pull(i, _):
             for u in range(UNROLL):
                 leaf = i * UNROLL + u
                 leaf_sums(leaf, sums, leaf)
-            return carry
+            return _
 
         lax.fori_loop(0, leaves // UNROLL, pull, 0)
         total, *moments = gathered(sums, leaves)
@@ -247,10 +260,12 @@
             in_specs=[vmem] * 5 + [smem] * 2,
             out_specs=(vmem, vmem),
             scratch_shapes=[
-                pltpu.VMEM((slots * ROWS, lanes), f32),
-                pltpu.VMEM((slots, ROWS, lanes), jnp.bfloat16),
+                pltpu.VMEM((slots * PAIR_ROWS, lanes), f32),
+                pltpu.VMEM((slots * SUM_ROWS, lanes), f32),
+                pltpu.VMEM((slots, lanes, lanes), jnp.bfloat16),
+                pltpu.VMEM((slots, SUM_ROWS, lanes), jnp.bfloat16),
                 pltpu.VMEM((leaves * PAIR_ROWS, lanes), f32),
-                pltpu.VMEM((leaves, lanes, PAIR_ROWS), jnp.bfloat16),
+                pltpu.VMEM((leaves, PAIR_ROWS, lanes), jnp.bfloat16),
                 pltpu.VMEM((leaves * SUM_ROWS, lanes), f32),
                 pltpu.VMEM((lent * SUM_ROWS, lanes), f32),
                 pltpu.VMEM((3, lent, lanes), f32),

time: 148 us -> 91.2 us (0.62)
  Pallas kernels: 141 us -> 84.4 us
    pallas_call x1, Pallas kernels: 141 us -> 84.4 us  [body(): pl.pallas_call(functools.partial(kernel, sizes), out_shape=(state, state)...]
where the time goes in v1:
time: 91.2 us; the launch traced here: 91 us
  Pallas kernels  84.4 us (93%)
  local copies, waits for them, and re-layouts  5.31 us (6%)
  between operations  1.32 us (1%)
    pallas_call x1, Pallas kernels, body(): pl.pallas_call(functools.partial(kernel, sizes), out_shape=(state, state)...  84.4 us
    unnamed x9, local copies, waits for them, and re-layouts  3.94 us

profile of v1, /device:TPU:0, one launch (start us, length us, event | category | flops | bytes accessed | tf_op | source)
XLA Modules:
  0.0 91.0 jit_solution(950413584380088890)
XLA Ops:
  1.3 0.0 copy-start
  1.3 0.0 copy-start.1
  1.3 0.7 broadcast_in_dim.2.live_in
  2.0 1.6 %copy.21 = f32[1,3,64,128]{3,2,1,0:T(8,128)} copy(f32[1,3,64,128]{3,1,2,0:T(4,128)} %bitcast.24) | data formatting | bytes 196608
  3.5 0.0 copy-done
  3.5 0.0 copy-done.1
  3.5 0.7 copy_bitcast_fusion.2
  4.2 84.4 %shard_map.86 = (f32[3,64,128]{2,1,0:T(8,128)}, f32[3,64,128]{2,1,0:T(8,128)}) custom-call(f32[3,64,128]{2,1,0:T(8,128)} %bitcast.21, f32[3,64,128]{2,1,0:T(8,128)} %get-tuple-element.7.v_in, f32[64,128]{1,0:T(8,128)} %bitcast.29, f32[3,64,128]{2,1,0:T(8,128)} %get-tuple-element.6.kick, f32[64,128]{1,0:T(8,128)} %broadcast_in_dim.2.live_in, s32[8,64]{1,0:T(8,128)} %lists.1, ...), custom_call_target="tpu_custom_call" | custom-call | tf_op jit(solution)/shard_map/pallas_call | solution.py:257
  88.6 0.0 copy-start.2
  88.6 1.7 %copy.19 = f32[1,3,64,128]{3,1,2,0:T(4,128)} copy(f32[1,3,64,128]{3,2,1,0:T(8,128)} %bitcast.28) | data formatting | bytes 196608
  90.3 0.0 copy-done.2
  90.3 0.7 copy.20
  (1 shorter events, 0.0 us)
Async XLA Ops:
  1.3 2.3 %copy-start = (f32[3,8192]{1,0:T(4,128)S(1)}, f32[3,8192]{1,0:T(4,128)}, u32[]{:S(2)}) copy-start(f32[3,8192]{1,0:T(4,128)} %param.10) | copy-start | bytes 294916
  1.3 2.2 %copy-start.1 = (f32[3,8192]{1,0:T(4,128)S(1)}, f32[3,8192]{1,0:T(4,128)}, u32[]{:S(2)}) copy-start(f32[3,8192]{1,0:T(4,128)} %param.8) | copy-start | bytes 294916
  88.6 1.7 %copy-start.2 = (f32[3,64,128]{2,1,0:T(8,128)S(1)}, f32[3,64,128]{2,1,0:T(8,128)}, u32[]{:S(2)}) copy-start(f32[3,64,128]{2,1,0:T(8,128)} %get-tuple-element.4) | copy-start | bytes 294916

commit v2 on v1

v2 whole, which is shorter than its diff:
```python
import functools

import jax
import jax.numpy as jnp
from jax import lax
from jax.experimental import pallas as pl
from jax.experimental.pallas import tpu as pltpu
from jax.sharding import PartitionSpec as P

SUBCYCLES = 4

soften_sq = 0.04
cutoff_sq = 9.0
time_step = 0.5

MESH = pl.DeviceIdType.MESH
COMPS = 4
PAIR = 2 * COMPS
GROUP = 4
SUM_ROWS = 16
TARGET_ROWS = 8 * PAIR
UNROLL = 16
ROUND_UP = 1.0 + 2.0**-22
WAYS = [(a, b) for a in (-1, 0, 1) for b in (-1, 0, 1)]
BESIDE = [way for way in WAYS if way != (0, 0)]


def thirds(value):
    first = value.astype(jnp.bfloat16).astype(jnp.float32)
    rest = value - first
    second = rest.astype(jnp.bfloat16).astype(jnp.float32)
    return first, second, rest - second


def slot_of(a, b):
    return (a + 1) * 3 + b + 1


def kernel(
    sizes, p_in, v_in, mass, kick_in, lists, ghosts, count, p_out, v_out,
    p, v, kick, pool, carry, narrow, sums, ghost_sums, ghost_v, ghost_kick, sent, got,
    send_sem, recv_sem,
):
    nx, ny = sizes
    leaves, lanes = mass.shape
    entries = lists.shape[0]
    lent = ghosts.shape[0]
    me_x, me_y = lax.axis_index("gx"), lax.axis_index("gy")

    def device(a, b):
        return (lax.rem(me_x + (a + nx), nx), lax.rem(me_y + (b + ny), ny))

    barrier = pltpu.get_barrier_semaphore()
    for a, b in BESIDE:
        pl.semaphore_signal(barrier, inc=1, device_id=device(a, b), device_id_type=MESH)

    def rows_of(index, height):
        return pl.ds(pl.multiple_of(index * height, height), height)

    for g in range(lent):
        leaf = ghosts[g]
        at = pl.ds(g * COMPS, 3)
        last = pl.ds(g * COMPS + 3, 1)
        sent[0, at, :] = p_in[leaf]
        sent[0, last, :] = mass[pl.ds(leaf, 1), :]
        ghost_v[at, :] = v_in[leaf]
        ghost_v[last, :] = jnp.zeros((1, lanes), jnp.float32)
        ghost_kick[at, :] = kick_in[leaf]
        ghost_kick[last, :] = jnp.zeros((1, lanes), jnp.float32)

    def copies(k):
        made = []
        for a, b in BESIDE:
            made.append(
                pltpu.make_async_remote_copy(
                    src_ref=sent.at[k],
                    dst_ref=got.at[k, slot_of(-a, -b)],
                    send_sem=send_sem.at[k, slot_of(a, b)],
                    recv_sem=recv_sem.at[k, slot_of(-a, -b)],
                    device_id=device(a, b),
                    device_id_type=MESH,
                )
            )
        return made

    pl.semaphore_wait(barrier, len(BESIDE))
    for copy in copies(0):
        copy.start()

    for leaf in range(leaves):
        at = pl.ds(leaf * COMPS, 3)
        last = pl.ds(leaf * COMPS + 3, 1)
        p[at, :] = p_in[leaf]
        p[last, :] = mass[pl.ds(leaf, 1), :]
        v[at, :] = v_in[leaf]
        v[last, :] = jnp.zeros((1, lanes), jnp.float32)
        kick[at, :] = kick_in[leaf]
        kick[last, :] = jnp.zeros((1, lanes), jnp.float32)

    row = lax.broadcasted_iota(jnp.int32, (PAIR, lanes), 0)
    comp = row % COMPS
    former = row < COMPS
    weigh = comp == COMPS - 1
    zeros = jnp.zeros((PAIR, lanes), jnp.float32)
    ones = jnp.ones((PAIR, lanes), jnp.float32)
    lane = lax.broadcasted_iota(jnp.int32, (lanes, lanes), 1)
    quarter = lane // TARGET_ROWS * 2 + lane % PAIR // COMPS
    keep = [(quarter == g).astype(jnp.float32).astype(jnp.bfloat16) for g in range(GROUP)]
    blank = jnp.zeros((lanes, lanes), jnp.bfloat16)
    moving = jnp.where(weigh, 0.0, time_step)

    def roll(value, by):
        return pltpu.roll(value, by, 0)

    def all_rows(value):
        filled = jnp.where(comp == 0, roll(value, PAIR - 3), value)
        filled = jnp.where(comp == 1, roll(value, PAIR - 2), filled)
        return jnp.where(comp == 2, roll(value, PAIR - 1), filled)

    def halves(value):
        swapped = roll(value, COMPS)
        return jnp.where(former, value, swapped), jnp.where(former, swapped, value)

    def spread(place):
        scaled = place * (cutoff_sq**-0.5)
        square = scaled * scaled
        norm = (roll(square, 1) + (roll(square, 2) + roll(square, 3))) * ROUND_UP
        return thirds(jnp.where(weigh, -norm, scaled)), norm

    def lay_group(i, places, aims):
        tiles = []
        for j, place in enumerate(places):
            (one, two, three), norm = spread(place)
            tiles += [one, two, one, three, one, two, ones, zeros]
            heavy = all_rows(place) * (cutoff_sq**-1.5)
            moments = thirds(heavy * jnp.where(weigh, 1.0, place))
            firsts, seconds, rests = [halves(moment) for moment in moments]
            for h in range(2):
                top = jnp.where(former, firsts[h], seconds[h])
                low = jnp.where(former, rests[h], 0.0)
                carry[i * GROUP + 2 * j + h] = jnp.concatenate([top, low], axis=0).astype(jnp.bfloat16)
            if aims:
                base = thirds(all_rows(1.0 - norm))
                base = jnp.where(comp == 0, base[0], jnp.where(comp == 1, base[1], base[2]))
                aim = (
                    jnp.where(weigh, 1.0, 2.0 * one),
                    jnp.where(weigh, 0.0, 2.0 * two),
                    jnp.where(weigh, 0.0, 2.0 * three),
                    jnp.where(weigh, 0.0, base),
                )
                aim = [halves(part) for part in aim]
                for h in range(2):
                    a, b, c, d = [part[h] for part in aim]
                    narrow[i * GROUP + 2 * j + h] = jnp.concatenate(
                        [a, a, b, a, c, b, d, zeros], axis=0
                    ).astype(jnp.bfloat16)
        block = jnp.concatenate(tiles, axis=0).T.astype(jnp.bfloat16)
        for g in range(GROUP):
            pool[i * GROUP + g] = block * keep[g]

    def leaf_sums(leaf, out, where):
        near = [lists[e, leaf] for e in range(entries)]
        target = jnp.concatenate([narrow[leaf]] * 2, axis=0)
        pair = jnp.concatenate(
            [
                jnp.concatenate([target, blank], axis=1),
                jnp.concatenate([blank, target], axis=1),
            ],
            axis=0,
        )
        total = None
        for j in range(0, entries, 2):
            source = jnp.concatenate([pool[near[j]], pool[near[j + 1]]], axis=1)
            inside = jnp.dot(source, pair, preferred_element_type=jnp.float32)
            parts = []
            for half in range(2):
                close = inside[:, half * lanes : (half + 1) * lanes]
                inverse = lax.rsqrt((1.0 + soften_sq / cutoff_sq) - close)
                taper = jnp.maximum(close * inverse, 0.0)
                weight = taper * taper * inverse
                high = weight.astype(jnp.bfloat16)
                low = (weight - high.astype(jnp.float32)).astype(jnp.bfloat16)
                parts.append(jnp.concatenate([high, low], axis=1))
            moments = jnp.concatenate([carry[near[j]], carry[near[j + 1]]], axis=1)
            part = jnp.dot(
                moments, jnp.concatenate(parts, axis=0), preferred_element_type=jnp.float32
            )
            total = part if total is None else total + part
        out[rows_of(where, SUM_ROWS), :] = total[:, :lanes] + total[:, lanes:]

    def pull_of(out, first, second, place):
        sides = []
        for where in (first, second):
            both = out[rows_of(where * 2, PAIR), :] + out[rows_of(where * 2 + 1, PAIR), :]
            sides.append(both + roll(both, COMPS))
        moment = jnp.where(former, sides[0], sides[1])
        return moment - all_rows(moment) * place

    def lay_own(i, _):
        lay_group(i, [p[rows_of(2 * i + j, PAIR), :] for j in range(2)], True)
        return _

    def lay_lent(ref, at):
        for i in range(lent // GROUP):
            lay_group(
                leaves // GROUP + at * (lent // GROUP) + i,
                [ref[rows_of(2 * i + j, PAIR), :] for j in range(2)],
                False,
            )

    def pull(i, _):
        for u in range(UNROLL):
            leaf_sums(i * UNROLL + u, sums, i * UNROLL + u)
        return _

    def subcycle(k, lend):
        lax.fori_loop(0, leaves // GROUP, lay_own, 0, unroll=8)
        lay_lent(sent.at[k], slot_of(0, 0))
        for copy in copies(k):
            copy.wait_recv()
        for a, b in BESIDE:
            lay_lent(got.at[k, slot_of(a, b)], slot_of(a, b))
        if lend:
            for g in range(lent):
                leaf_sums(ghosts[g], ghost_sums, g)
            for g in range(0, lent, 2):
                rows = pl.ds(g * COMPS, PAIR)
                place = sent[k, rows, :]
                speed = ghost_v[rows, :] + moving * (
                    pull_of(ghost_sums, g, g + 1, place) + ghost_kick[rows, :]
                )
                ghost_v[rows, :] = speed
                sent[k + 1, rows, :] = place + moving * speed
            for copy in copies(k + 1):
                copy.start()
        lax.fori_loop(0, leaves // UNROLL, pull, 0)
        for leaf in range(0, leaves, 2):
            rows = pl.ds(leaf * COMPS, PAIR)
            place = p[rows, :]
            live = jnp.where(leaf + row // COMPS < count[0], moving, 0.0)
            speed = v[rows, :] + live * (pull_of(sums, leaf, leaf + 1, place) + kick[rows, :])
            v[rows, :] = speed
            p[rows, :] = place + live * speed

    def early(k, _):
        subcycle(k, True)
        return _

    lax.fori_loop(0, SUBCYCLES - 1, early, 0)
    subcycle(SUBCYCLES - 1, False)

    for leaf in range(leaves):
        at = pl.ds(leaf * COMPS, 3)
        p_out[leaf] = p[at, :]
        v_out[leaf] = v[at, :]

    for k in range(SUBCYCLES):
        for copy in copies(k):
            copy.wait_send()


def solution(mesh):
    sizes = (mesh.shape["gx"], mesh.shape["gy"])

    def body(positions, velocities, masses, long_kick, leaf_lists, ghost_ids, leaf_counts):
        leaves = leaf_lists.shape[1]
        lanes = masses.shape[0] // leaves
        lent = ghost_ids.shape[0]
        slots = leaves + len(WAYS) * lent
        state = jax.ShapeDtypeStruct((leaves, 3, lanes), jnp.float32)
        vmem = pl.BlockSpec(memory_space=pltpu.VMEM)
        smem = pl.BlockSpec(memory_space=pltpu.SMEM)
        f32 = jnp.float32

        def by_leaf(array):
            return array.reshape(3, leaves, lanes).transpose(1, 0, 2)

        places, speeds = pl.pallas_call(
            functools.partial(kernel, sizes),
            out_shape=(state, state),
            in_specs=[vmem] * 4 + [smem] * 3,
            out_specs=(vmem, vmem),
            scratch_shapes=[
                pltpu.VMEM((leaves * COMPS, lanes), f32),
                pltpu.VMEM((leaves * COMPS, lanes), f32),
                pltpu.VMEM((leaves * COMPS, lanes), f32),
                pltpu.VMEM((slots, lanes, lanes), jnp.bfloat16),
                pltpu.VMEM((slots, SUM_ROWS, lanes), jnp.bfloat16),
                pltpu.VMEM((leaves, TARGET_ROWS, lanes), jnp.bfloat16),
                pltpu.VMEM((leaves * SUM_ROWS, lanes), f32),
                pltpu.VMEM((lent * SUM_ROWS, lanes), f32),
                pltpu.VMEM((lent * COMPS, lanes), f32),
                pltpu.VMEM((lent * COMPS, lanes), f32),
                pltpu.VMEM((SUBCYCLES, lent * COMPS, lanes), f32),
                pltpu.VMEM((SUBCYCLES, len(WAYS), lent * COMPS, lanes), f32),
                pltpu.SemaphoreType.DMA((SUBCYCLES, len(WAYS))),
                pltpu.SemaphoreType.DMA((SUBCYCLES, len(WAYS))),
            ],
            compiler_params=pltpu.CompilerParams(collective_id=0, has_side_effects=True),
        )(
            by_leaf(positions),
            by_leaf(velocities),
            masses.reshape(leaves, lanes),
            by_leaf(long_kick),
            leaf_lists,
            ghost_ids,
            leaf_counts,
        )

        def by_part(array):
            return array.transpose(1, 0, 2).reshape(3, leaves * lanes)

        return by_part(places), by_part(speeds)

    return jax.shard_map(
        body,
        mesh=mesh,
        in_specs=(
            P(None, ("gx", "gy")),
            P(None, ("gx", "gy")),
            P(("gx", "gy")),
            P(None, ("gx", "gy")),
            P(None, ("gx", "gy")),
            P(("gx", "gy")),
            P(("gx", "gy")),
        ),
        out_specs=(P(None, ("gx", "gy")), P(None, ("gx", "gy"))),
        check_vma=False,
    )
```

time: 91.2 us -> 70.2 us (0.77)
  Pallas kernels: 84.4 us -> 66.4 us
  local copies, waits for them, and re-layouts: 5.31 us -> 2.28 us
    pallas_call x1, Pallas kernels: 84.4 us -> 66.4 us  [body(): pl.pallas_call(functools.partial(kernel, sizes), out_shape=(state, state)...]
    unnamed x9 -> x4, local copies, waits for them, and re-layouts: 3.94 us -> 2.28 us
where the time goes in v2:
time: 70.2 us; the launch traced here: 70 us
  Pallas kernels  66.4 us (95%)
  local copies, waits for them, and re-layouts  2.28 us (3%)
  between operations  1.3 us (2%)
    pallas_call x1, Pallas kernels, body(): pl.pallas_call(functools.partial(kernel, sizes), out_shape=(state, state)...  66.4 us
    unnamed x4, local copies, waits for them, and re-layouts  2.28 us

profile of v2, /device:TPU:0, one launch (start us, length us, event | category | flops | bytes accessed | tf_op | source)
XLA Modules:
  0.0 70.0 jit_solution(6313214866076135444)
XLA Ops:
  1.3 66.4 %shard_map.86 = (f32[64,3,128]{2,1,0:T(4,128)}, f32[64,3,128]{2,1,0:T(4,128)}) custom-call(f32[64,3,128]{2,1,0:T(4,128)} %bitcast.16, f32[64,3,128]{2,1,0:T(4,128)} %bitcast.17, f32[64,128]{1,0:T(8,128)} %bitcast.21, f32[64,3,128]{2,1,0:T(4,128)} %bitcast.18, s32[8,64]{1,0:T(8,128)} %lists.1, s32[8]{0:T(128)} %ghosts.1, s32[1]{0:T(128)S(6)} %copy.11.count), custom_call_target="tpu_custom_call" | custom-call | tf_op jit(solution)/shard_map/pallas_call | solution.py:278
  67.7 0.0 copy-start
  67.7 1.6 %copy.12 = f32[3,8192]{1,0:T(4,128)} copy(f32[3,8192]{1,0:T(4,128)} %bitcast.20) | data formatting | bytes 196608
  69.3 0.0 copy-done
  69.3 0.7 copy.13
Async XLA Ops:
  67.7 1.6 %copy-start = (f32[64,3,128]{2,1,0:T(4,128)S(1)}, f32[64,3,128]{2,1,0:T(4,128)}, u32[]{:S(2)}) copy-start(f32[64,3,128]{2,1,0:T(4,128)} %get-tuple-element.5) | copy-start | bytes 294916

commit v3 on v2

--- a/solution.py
+++ b/solution.py
@@ -19,7 +19,6 @@
 GROUP = 4
 SUM_ROWS = 16
 TARGET_ROWS = 8 * PAIR
-UNROLL = 16
 ROUND_UP = 1.0 + 2.0**-22
 WAYS = [(a, b) for a in (-1, 0, 1) for b in (-1, 0, 1)]
 BESIDE = [way for way in WAYS if way != (0, 0)]
@@ -38,7 +37,7 @@
 
 def kernel(
     sizes, p_in, v_in, mass, kick_in, lists, ghosts, count, p_out, v_out,
-    p, v, kick, pool, carry, narrow, sums, ghost_sums, ghost_v, ghost_kick, sent, got,
+    p, v, kick, pool, carry, narrow, sums, ghost_v, ghost_kick, sent, got,
     send_sem, recv_sem,
 ):
     nx, ny = sizes
@@ -86,6 +85,34 @@
     pl.semaphore_wait(barrier, len(BESIDE))
     for copy in copies(0):
         copy.start()
+
+    def flag(truth):
+        return truth.astype(jnp.int32)
+
+    ids = [ghosts[g] for g in range(lent)]
+    new = []
+    for g in range(lent):
+        found = jnp.int32(1)
+        for h in range(g):
+            found = found * (1 - flag(ids[h] == ids[g]))
+        new.append(found)
+    total = sum(new)
+    place_lent = [sum(new[h] * flag(ids[h] < ids[g]) for h in range(lent)) for g in range(lent)]
+    order, place_of = [], []
+    for s in range(leaves):
+        leaf = s - total
+        for g in range(lent):
+            leaf = leaf + new[g] * flag(ids[g] - place_lent[g] <= s - total)
+        if s < lent:
+            for g in range(lent):
+                leaf = leaf + new[g] * flag(place_lent[g] == s) * (ids[g] - leaf)
+        order.append(leaf)
+        place = total + s
+        for g in range(lent):
+            place = place - new[g] * flag(ids[g] < s)
+        for g in range(lent):
+            place = place + new[g] * flag(ids[g] == s) * (place_lent[g] - place)
+        place_of.append(place)
 
     for leaf in range(leaves):
         at = pl.ds(leaf * COMPS, 3)
@@ -186,12 +213,13 @@
                 moments, jnp.concatenate(parts, axis=0), preferred_element_type=jnp.float32
             )
             total = part if total is None else total + part
-        out[rows_of(where, SUM_ROWS), :] = total[:, :lanes] + total[:, lanes:]
+        out[where] = total[:, :lanes] + total[:, lanes:]
 
     def pull_of(out, first, second, place):
         sides = []
         for where in (first, second):
-            both = out[rows_of(where * 2, PAIR), :] + out[rows_of(where * 2 + 1, PAIR), :]
+            tile = out[where]
+            both = tile[:PAIR] + tile[PAIR:]
             sides.append(both + roll(both, COMPS))
         moment = jnp.where(former, sides[0], sides[1])
         return moment - all_rows(moment) * place
@@ -208,53 +236,49 @@
                 False,
             )
 
-    def pull(i, _):
-        for u in range(UNROLL):
-            leaf_sums(i * UNROLL + u, sums, i * UNROLL + u)
-        return _
-
-    def subcycle(k, lend):
+    def pull(slots):
+        for s in slots:
+            leaf_sums(order[s], sums, s)
+
+    def subcycle(k, carried):
         lax.fori_loop(0, leaves // GROUP, lay_own, 0, unroll=8)
         lay_lent(sent.at[k], slot_of(0, 0))
         for copy in copies(k):
             copy.wait_recv()
         for a, b in BESIDE:
             lay_lent(got.at[k, slot_of(a, b)], slot_of(a, b))
-        if lend:
-            for g in range(lent):
-                leaf_sums(ghosts[g], ghost_sums, g)
-            for g in range(0, lent, 2):
-                rows = pl.ds(g * COMPS, PAIR)
-                place = sent[k, rows, :]
-                speed = ghost_v[rows, :] + moving * (
-                    pull_of(ghost_sums, g, g + 1, place) + ghost_kick[rows, :]
-                )
-                ghost_v[rows, :] = speed
-                sent[k + 1, rows, :] = place + moving * speed
-            for copy in copies(k + 1):
-                copy.start()
-        lax.fori_loop(0, leaves // UNROLL, pull, 0)
+        pull(range(lent))
+        for g in range(0, lent, 2):
+            rows = pl.ds(g * COMPS, PAIR)
+            place = sent[k, rows, :]
+            speed = ghost_v[rows, :] + moving * (
+                pull_of(sums, place_lent[g], place_lent[g + 1], place) + ghost_kick[rows, :]
+            )
+            ghost_v[rows, :] = speed
+            sent[k + 1, rows, :] = place + moving * speed
+        for copy in copies(k + 1):
+            copy.start()
+        pull(range(lent, leaves))
         for leaf in range(0, leaves, 2):
             rows = pl.ds(leaf * COMPS, PAIR)
             place = p[rows, :]
             live = jnp.where(leaf + row // COMPS < count[0], moving, 0.0)
-            speed = v[rows, :] + live * (pull_of(sums, leaf, leaf + 1, place) + kick[rows, :])
+            accel = pull_of(sums, place_of[leaf], place_of[leaf + 1], place)
+            speed = v[rows, :] + live * (accel + kick[rows, :])
             v[rows, :] = speed
             p[rows, :] = place + live * speed
-
-    def early(k, _):
-        subcycle(k, True)
-        return _
-
-    lax.fori_loop(0, SUBCYCLES - 1, early, 0)
-    subcycle(SUBCYCLES - 1, False)
+        return carried
+
+    lax.fori_loop(0, SUBCYCLES, subcycle, 0)
 
     for leaf in range(leaves):
         at = pl.ds(leaf * COMPS, 3)
         p_out[leaf] = p[at, :]
         v_out[leaf] = v[at, :]
 
-    for k in range(SUBCYCLES):
+    for copy in copies(SUBCYCLES):
+        copy.wait_recv()
+    for k in range(SUBCYCLES + 1):
         for copy in copies(k):
             copy.wait_send()
 
@@ -287,14 +311,13 @@
                 pltpu.VMEM((slots, lanes, lanes), jnp.bfloat16),
                 pltpu.VMEM((slots, SUM_ROWS, lanes), jnp.bfloat16),
                 pltpu.VMEM((leaves, TARGET_ROWS, lanes), jnp.bfloat16),
-                pltpu.VMEM((leaves * SUM_ROWS, lanes), f32),
-                pltpu.VMEM((lent * SUM_ROWS, lanes), f32),
+                pltpu.VMEM((leaves, SUM_ROWS, lanes), f32),
                 pltpu.VMEM((lent * COMPS, lanes), f32),
                 pltpu.VMEM((lent * COMPS, lanes), f32),
-                pltpu.VMEM((SUBCYCLES, lent * COMPS, lanes), f32),
-                pltpu.VMEM((SUBCYCLES, len(WAYS), lent * COMPS, lanes), f32),
-                pltpu.SemaphoreType.DMA((SUBCYCLES, len(WAYS))),
-                pltpu.SemaphoreType.DMA((SUBCYCLES, len(WAYS))),
+                pltpu.VMEM((SUBCYCLES + 1, lent * COMPS, lanes), f32),
+                pltpu.VMEM((SUBCYCLES + 1, len(WAYS), lent * COMPS, lanes), f32),
+                pltpu.SemaphoreType.DMA((SUBCYCLES + 1, len(WAYS))),
+                pltpu.SemaphoreType.DMA((SUBCYCLES + 1, len(WAYS))),
             ],
             compiler_params=pltpu.CompilerParams(collective_id=0, has_side_effects=True),
         )(

time: 70.2 us -> 64.5 us (0.919)
  Pallas kernels: 66.4 us -> 60.8 us
    pallas_call x1, Pallas kernels: 66.4 us -> 60.8 us  [body(): pl.pallas_call(functools.partial(kernel, sizes), out_shape=(state, state)...]
where the time goes in v3:
time: 64.5 us; the launch traced here: 64.4 us
  Pallas kernels  60.8 us (94%)
  local copies, waits for them, and re-layouts  2.28 us (4%)
  between operations  1.3 us (2%)
    pallas_call x1, Pallas kernels, body(): pl.pallas_call(functools.partial(kernel, sizes), out_shape=(state, state)...  60.8 us
    unnamed x4, local copies, waits for them, and re-layouts  2.28 us

profile of v3, /device:TPU:0, one launch (start us, length us, event | category | flops | bytes accessed | tf_op | source)
XLA Modules:
  0.0 64.4 jit_solution(6987534796879302234)
XLA Ops:
  1.3 60.8 %shard_map.86 = (f32[64,3,128]{2,1,0:T(4,128)}, f32[64,3,128]{2,1,0:T(4,128)}) custom-call(f32[64,3,128]{2,1,0:T(4,128)} %bitcast.16, f32[64,3,128]{2,1,0:T(4,128)} %bitcast.17, f32[64,128]{1,0:T(8,128)} %bitcast.21, f32[64,3,128]{2,1,0:T(4,128)} %bitcast.18, s32[8,64]{1,0:T(8,128)} %lists.1, s32[8]{0:T(128)} %ghosts.1, s32[1]{0:T(128)S(6)} %copy.11.count), custom_call_target="tpu_custom_call" | custom-call | tf_op jit(solution)/shard_map/pallas_call | solution.py:302
  62.1 0.0 copy-start
  62.1 1.6 %copy.12 = f32[3,8192]{1,0:T(4,128)} copy(f32[3,8192]{1,0:T(4,128)} %bitcast.20) | data formatting | bytes 196608
  63.7 0.0 copy-done
  63.7 0.7 %copy.13 = f32[3,8192]{1,0:T(4,128)} copy(f32[3,8192]{1,0:T(4,128)S(1)} %bitcast.19) | data formatting | bytes 196608
Async XLA Ops:
  62.1 1.6 %copy-start = (f32[64,3,128]{2,1,0:T(4,128)S(1)}, f32[64,3,128]{2,1,0:T(4,128)}, u32[]{:S(2)}) copy-start(f32[64,3,128]{2,1,0:T(4,128)} %get-tuple-element.5) | copy-start | bytes 294916
